TPU v7x, 32 devices: a whole 2x2x4 slice. The times are simulated.
32 devices in a mesh: dp: 8 (over z, y), mp: 4 (over x, core).
Axes of the slice: x: 2, y: 2, z: 4, core: 2. Of those that a mesh axis runs over, the one named last changes fastest.
Arguments:
- queries: bfloat16 [256, 64, 128], P('dp', 'mp'), may hold values from -8 to 8
- lookup_sheets: bfloat16 [8192, 16, 8, 128], P('dp', None, 'mp'), may hold values from -6 to 6
- content_sheets: bfloat16 [8192, 16, 8, 128], P('dp', None, 'mp'), may hold values from -12 to 12
- page_table: int32 [256, 32], replicated, may hold values from 0 to 8191, as said below
- context_len: int32 [256], replicated, may hold values from 32 to 512, as said below
- out_weight: bfloat16 [8192, 8192], P('mp', 'dp'), may hold values from -0.0625 to 0.0625
Outputs:
- attention: bfloat16 [256, 64, 128], P('dp', 'mp')
- projected: bfloat16 [256, 8192], P('mp', 'dp')
Inputs may be any that keep to these rules, and one draw needn't show every extreme that they name: `page_table`: every entry names a pool page, 0 to 8191, and every pool page appears exactly once in the whole table. `context_len`: each length lies between 32 and 512; most contexts are short, and some request has exactly 512 tokens.
All inputs are finite; a program needn't handle non-finite values.
Results may differ from a plain program's by a relative error of at most 0.0015.
Values may be sent and summed in bfloat16 or wider, within the bound.
A program may use at most 128 MiB of HBM per device.

v0:
```python
import jax
import jax.numpy as jnp
from jax import lax
from jax.sharding import PartitionSpec as P


def for_sending(array):
    return jax.tree.map(lambda a: a.astype(jnp.bfloat16) if a.dtype == jnp.float32 else a, array)


def pick_rows(onehot_f, table):
    flat = table.reshape(table.shape[0], -1)
    picked = jnp.dot(
        onehot_f, flat, preferred_element_type=jnp.float32, precision=lax.Precision.HIGHEST
    )
    return picked.reshape((onehot_f.shape[0],) + table.shape[1:])


def sum_rows(onehot_t, table):
    flat = table.reshape(table.shape[0], -1)
    summed = jnp.dot(
        onehot_t, flat, preferred_element_type=jnp.float32, precision=lax.Precision.HIGHEST
    )
    return summed.reshape((onehot_t.shape[0],) + table.shape[1:])


def shards(queries, lookup_sheets, content_sheets, page_table, context_len, out_weight):
    req_rows = page_table.shape[0]
    max_pages = page_table.shape[1]
    pool_local, page_len, kv_local, head_dim = lookup_sheets.shape
    q_local = queries.shape[1]
    cluster_member = q_local // kv_local
    dp_count = lax.axis_size("dp")
    rows_mine = req_rows // dp_count
    first_page = lax.axis_index("dp") * pool_local
    local_ids = first_page + jnp.arange(pool_local, dtype=jnp.int32)
    table_blocks = page_table.reshape(dp_count, rows_mine, max_pages)
    block_starts = jnp.arange(dp_count, dtype=jnp.int32) * rows_mine
    row_numbers = jnp.arange(rows_mine, dtype=jnp.int32)
    column_numbers = jnp.arange(max_pages, dtype=jnp.int32)

    def find_owner(carry, inputs):
        table_block, block_start = inputs
        matched = (table_block[None, :, :] == local_ids[:, None, None]).astype(jnp.int32)
        owner_add = jnp.sum(matched * (block_start + row_numbers)[None, :, None], axis=(1, 2))
        slot_add = jnp.sum(matched * column_numbers[None, None, :], axis=(1, 2))
        return ((carry[0] + owner_add, carry[1] + slot_add), None)

    zeros_local = jnp.zeros((pool_local,), jnp.int32)
    (owners, page_slot), unused = lax.scan(
        find_owner, (zeros_local, zeros_local), (table_blocks, block_starts)
    )
    onehot = owners[:, None] == jnp.arange(req_rows, dtype=jnp.int32)[None, :]
    onehot_f = onehot.astype(jnp.float32)
    onehot_t = jnp.transpose(onehot_f)
    all_queries = lax.all_gather(queries, "dp", axis=0, tiled=True)
    page_queries = jnp.dot(
        onehot.astype(jnp.bfloat16),
        all_queries.reshape(req_rows, q_local * head_dim),
        preferred_element_type=jnp.float32,
    ).astype(jnp.bfloat16)
    page_queries = page_queries.reshape(pool_local, kv_local, cluster_member, head_dim)
    scores = jnp.einsum(
        "pkgd,ptkd->pkgt", page_queries, lookup_sheets, preferred_element_type=jnp.float32
    ) * head_dim ** (-0.5)
    page_length = jnp.sum(jnp.where(onehot, context_len[None, :], 0), axis=1)
    position = page_slot[:, None] * page_len + jnp.arange(page_len, dtype=jnp.int32)[None, :]
    is_valid = (position < page_length[:, None])[:, None, None, :]
    scores = jnp.where(is_valid, scores, -1e30)
    page_peak = jnp.max(scores, axis=3)
    weights = jnp.where(is_valid, jnp.exp(scores - page_peak[..., None]), 0.0)
    page_mass = jnp.sum(weights, axis=3)
    page_acc = jnp.einsum(
        "pkgt,ptkd->pkgd",
        weights.astype(jnp.bfloat16),
        content_sheets,
        preferred_element_type=jnp.float32,
    )
    local_peak = jnp.max(
        jnp.where(onehot[:, :, None, None], page_peak[:, None, :, :], -1e30), axis=0
    )
    peak_all = lax.pmax(for_sending(local_peak), "dp").astype(local_peak.dtype)
    factor = jnp.exp(page_peak - pick_rows(onehot_f, peak_all))
    mass_sum = sum_rows(onehot_t, page_mass * factor)
    acc_sum = sum_rows(onehot_t, page_acc * factor[..., None])
    acc_mine, mass_mine = (
        lax.psum_scatter(acc_sum, "dp", scatter_dimension=0, tiled=True),
        lax.psum_scatter(mass_sum, "dp", scatter_dimension=0, tiled=True),
    )
    attention = (
        (acc_mine / mass_mine[..., None]).astype(jnp.bfloat16).reshape(rows_mine, q_local, head_dim)
    )
    flat_attention = attention.reshape(rows_mine, q_local * head_dim)

    def project(block_rows):
        return jnp.dot(block_rows, out_weight, preferred_element_type=jnp.float32)

    partial_value = project(lax.all_gather(flat_attention, "dp", axis=0, tiled=True))
    projected = lax.psum_scatter(partial_value, "mp", scatter_dimension=0, tiled=True).astype(
        jnp.bfloat16
    )
    return (attention, projected)


def solution(mesh):
    placed = (
        P("dp", "mp", None),
        P("dp", None, "mp", None),
        P("dp", None, "mp", None),
        P(),
        P(),
        P("mp", "dp"),
    )
    return jax.shard_map(
        shards,
        mesh=mesh,
        in_specs=placed,
        out_specs=(P("dp", "mp", None), P("mp", "dp")),
        check_vma=False,
    )
```

profile of v0, /device:TPU:0, one launch (start us, length us, event | category | flops | bytes accessed | tf_op | source)
XLA Modules:
  0.0 334.4 jit_solution(1228513489586116770)
XLA Ops:
  8.0 0.9 copy.37
  8.8 18.3 %while.15 = (s32[]{:T(128)}, s32[1024]{0:T(1024)S(1)}, s32[1024]{0:T(1024)S(1)}, s32[8,32,32]{2,1,0:T(8,128)S(1)}, s32[8]{0:T(128)S(1)}, /*index=5*/s32[]{:T(128)}, s32[]{:T(128)}, s32[]{:T(128)}) while((s32[]{:T(128)}, s32[1024]{0:T(1024)S(1)}, s32[1024]{0:T(1024)S(1)}, s32[8,32,32]{2,1,0:T(8,128)S(1)}, ...), condition=%wide.region_3.4_spmd.clone.clone, body=%wide.region_0.3_spmd.clone.clone.sunk | while | flops 5245987 | bytes 53623 | solution.py:50
  14.8 0.8 fusion.49
  17.1 0.8 fusion.49
  23.9 0.8 fusion.49
  27.1 1.0 select_reduce_fusion.1
  28.7 24.8 %all-gather.3.cloned.1.call-done = bf16[256,16,128]{2,1,0:T(8,128)(2,1)} async-done(((bf16[32,16,128]{2,1,0:T(8,128)(2,1)}), bf16[256,16,128]{2,1,0:T(8,128)(2,1)}) %all-gather.3.cloned.1.call-update) | async-done | bytes 1048592 | tf_op jit(solution)/shard_map/all_gather | solution.py:56
  53.5 2.5 convert_bitcast_fusion
  56.0 1.4 copy.54
  57.4 9.5 %fusion.10 = (f32[1024,2,8]{2,1,0:T(2,128)S(1)}, f32[1024,2,8,16]{3,2,1,0:T(8,128)}) fusion(pred[1024,16]{1,0:T(8,128)(4,1)S(1)} %add_compare_fusion, bf16[1024,2,8,128]{3,2,1,0:T(8,128)(2,1)S(1)} %bitcast.65, bf16[1024,16,2,128]{3,2,1,0:T(2,128)(2,1)} %param.9), kind=kOutput, calls=%fused_computation.19 | convolution fusion | flops 67878912 | bytes 13713408 | tf_op jit(solution)/shard_map/pkgd,ptkd->pkgt/dot_general | solution.py:63
  67.3 5.9 %select_reduce_fusion = bf16[256,2,8]{0,2,1:T(8,128)(2,1)S(1)} fusion(f32[1024,2,8]{2,1,0:T(2,128)S(1)} %get-tuple-element.133, pred[1024,256]{1,0:T(8,128)(4,1)S(1)} %iota_compare_fusion), kind=kLoop, calls=%fused_computation.11 | loop fusion | flops 8384512 | bytes 335872 | tf_op jit(solution)/shard_map/reduce_max | solution.py:79
  73.2 19.4 %pmax.7 = bf16[2,8,256]{2,1,0:T(8,128)(2,1)S(1)} all-reduce(bf16[2,8,256]{2,1,0:T(8,128)(2,1)S(1)} %bitcast.71), channel_id=1, replica_groups=mesh['dp'=8,'mp'=4] {'dp'}, use_global_device_ids=true, to_apply=%region_7.8 | all-reduce | flops 4096 | bytes 16384 | tf_op jit(solution)/shard_map/pmax | solution.py:82
  92.7 30.0 %fusion.11 = f32[1024,2,8]{2,1,0:T(2,128)S(1)} fusion(f32[1024,2,8,16]{3,2,1,0:T(8,128)} %get-tuple-element.134, f32[1024,2,8]{2,1,0:T(2,128)S(1)} %get-tuple-element.133, pred[1024,16]{1,0:T(8,128)(4,1)S(1)} %add_compare_fusion), kind=kLoop, calls=%fused_computation.20 | loop fusion | flops 1294336 | bytes 1196032 | tf_op jit(solution)/shard_map/reduce_sum | solution.py:72
  125.3 12.5 %broadcast_multiply_fusion = f32[1024,2,8,128]{3,2,1,0:T(8,128)S(1)} fusion(f32[1024,2,8]{2,1,0:T(2,128)S(1)} %copy.41, bf16[1024,16,2,128]{3,2,1,0:T(2,128)(2,1)} %param.10, f32[1024,2,8,16]{3,2,1,0:T(8,128)} %get-tuple-element.134, f32[1024,2,8]{2,1,0:T(2,128)S(1)} %get-tuple-element.133, pred[1024,16]{1,0:T(8,128)(4,1)S(1)} %add_compare_fusion), kind=kOutput, calls=%fused_computation.22 | convolution fusion | flops 70516736 | bytes 17973248 | tf_op jit(solution)/shard_map/pkgt,ptkd->pkgd/dot_general | solution.py:73
  137.8 7.3 %copy.71 = f32[128,8,16,128]{3,1,2,0:T(8,128)} copy(f32[128,8,16,128]{3,2,1,0:T(8,128)S(1)} %bitcast.66) | data formatting | bytes 16777216
  145.1 9.3 %copy.42 = f32[2048,1024]{1,0:T(8,128)} copy(f32[2048,1024]{0,1:T(8,128)} %bitcast.64) | data formatting | bytes 16777216 | tf_op jit(solution)/shard_map/dot_general | solution.py:21
  154.4 8.2 %fusion.31 = f32[256,2,8,128]{3,0,2,1:T(8,128)} fusion(f32[2,8,128,1024]{3,2,1,0:T(8,128)} %bitcast.63, s32[1024]{0:T(1024)S(1)} %get-tuple-element.63), kind=kOutput, calls=%fused_computation.39 | convolution fusion | flops 6442975232 | bytes 10489856 | tf_op jit(solution)/shard_map/dot_general | solution.py:21
  162.7 21.9 %reduce-scatter.10.cloned.1.call-done = f32[32,16]{1,0:T(8,128)} async-done(((f32[256,16]{1,0:T(8,128)}), f32[32,16]{1,0:T(8,128)}) %reduce-scatter.10.cloned.1.call-update) | async-done | bytes 2064
  185.3 70.6 %reduce-scatter.6.cloned.1.call-done = f32[32,2,8,128]{3,0,2,1:T(8,128)} async-done(((f32[256,2,8,128]{3,0,2,1:T(8,128)}), f32[32,2,8,128]{3,0,2,1:T(8,128)}) %reduce-scatter.6.cloned.1.call-update) | async-done | bytes 262160 | tf_op jit(solution)/shard_map/reduce_scatter | solution.py:87
  256.0 1.1 divide_convert_fusion
  257.9 40.2 %all-gather.5.cloned.1.call-done = bf16[256,2048]{1,0:T(8,128)(2,1)} async-done(((bf16[32,2048]{1,0:T(8,128)(2,1)}), bf16[256,2048]{1,0:T(8,128)(2,1)}) %all-gather.5.cloned.1.call-update) | async-done | bytes 1048592 | tf_op jit(solution)/shard_map/all_gather | solution.py:98
  298.1 4.8 %fusion.42 = f32[256,1024]{1,0:T(8,128)} fusion(bf16[256,2048]{1,0:T(8,128)(2,1)} %all-gather.5.cloned.1.call-done, bf16[2048,1024]{1,0:T(8,128)(2,1)} %param.13), kind=kOutput, calls=%fused_computation.55 | convolution fusion | flops 1073741824 | bytes 6291456 | tf_op jit(solution)/shard_map/dot_general | solution.py:96
  303.6 22.6 %reduce-scatter.8.cloned.1.call-done = f32[64,1024]{1,0:T(8,128)} async-done(((f32[256,1024]{1,0:T(8,128)}), f32[64,1024]{1,0:T(8,128)}) %reduce-scatter.8.cloned.1.call-update) | async-done | bytes 262160 | tf_op jit(solution)/shard_map/reduce_scatter | solution.py:99
  326.2 1.6 convert_element_type.24
  (71 shorter events, 22.0 us)
Async XLA Ops:
  7.2 46.3 %all-gather.3.cloned.1.call-start = ((), (), s32[]{:S(2)}) async-start(), calls=%async_computation.3 | async-start | bytes 1179648 | tf_op jit(solution)/shard_map/all_gather | solution.py:56
  7.9 176.7 %reduce-scatter.10.cloned.1.call-start = ((), (), s32[]{:S(2)}) async-start(), calls=%async_computation.7 | async-start | bytes 147456
  125.3 130.7 %reduce-scatter.6.cloned.1.call-start = ((), (), s32[]{:S(2)}) async-start(), calls=%async_computation.4 | async-start | bytes 2359296 | tf_op jit(solution)/shard_map/reduce_scatter | solution.py:87
  162.6 135.5 %all-gather.5.cloned.1.call-start = ((), (), s32[]{:S(2)}) async-start(), calls=%async_computation.5 | async-start | bytes 1179648 | tf_op jit(solution)/shard_map/all_gather | solution.py:98
  257.8 68.4 %reduce-scatter.8.cloned.1.call-start = ((), (), s32[]{:S(2)}) async-start(), calls=%async_computation.6 | async-start | bytes 1310720 | tf_op jit(solution)/shard_map/reduce_scatter | solution.py:99
Sparse Core Ops, SparseCore 0:
  10.1 43.3 all-gather.2
  125.4 59.1 reduce-scatter.9
  188.1 67.8 reduce-scatter.5
  258.5 39.5 all-gather.4
  303.0 23.1 reduce-scatter.7
where the time goes:
time: 335 us; the launch traced here: 334 us
  waiting for transfers between devices  181 us (54%)
  other arithmetic  52.6 us (16%)
  matrix products  38.3 us (11%)
  local copies, waits for them, and re-layouts  28.6 us (9%)
  blocking collectives  19.4 us (6%)
  between operations  13.9 us (4%)
    reduce_scatter x1, waiting for transfers between devices, shards(): lax.psum_scatter(acc_sum, 'dp', scatter_dimension=0, tiled=True)  70.6 us
    all_gather x1, waiting for transfers between devices, shards(): lax.all_gather(flat_attention, 'dp', axis=0, tiled=True)  40.2 us
    reduce_sum x1, other arithmetic, shards(): page_mass = jnp.sum(weights, axis=3)  30 us
    all_gather x1, waiting for transfers between devices, shards(): all_queries = lax.all_gather(queries, 'dp', axis=0, tiled=True)  24.8 us
    reduce_scatter x1, waiting for transfers between devices, shards(): lax.psum_scatter(partial_value, 'mp', scatter_dimension=0, tiled=True)  22.6 us
    unnamed x6, waiting for transfers between devices  22.6 us
    pmax x1, blocking collectives, shards(): peak_all = lax.pmax(for_sending(local_peak), 'dp').astype(local_peak.dtype)  19.4 us
    unnamed x7, local copies, waits for them, and re-layouts  12.5 us
  transfers between devices with their start and end apart: 5, of which 5 were waited for; matrix products, arithmetic and copies ran while one was open for 18% of the time, Pallas kernels for 0%

commit v1 on v0

v1 whole, which is shorter than its diff:
```python
import functools

import jax
import jax.numpy as jnp
from jax import lax
from jax.experimental import pallas as pl
from jax.experimental.pallas import tpu as pltpu
from jax.sharding import PartitionSpec as P

MESH = pl.DeviceIdType.MESH
NEG = -1e30
DEPTH = 4
PRE = 2


def axis_barrier(axes):
    barrier = pltpu.get_barrier_semaphore()
    total = 0
    for name in axes:
        n = lax.axis_size(name)
        me = lax.axis_index(name)
        for step in range(1, n):
            pl.semaphore_signal(
                barrier, inc=1, device_id={name: lax.rem(me + step, n)}, device_id_type=MESH
            )
        total += n - 1
    pl.semaphore_wait(barrier, total)


def gather_kernel(q_ref, all_ref, send_sem, recv_sem, own_sem):
    n = lax.axis_size("dp")
    me = lax.axis_index("dp")
    axis_barrier(("dp",))
    copies = []
    for step in range(1, n):
        copy = pltpu.make_async_remote_copy(
            src_ref=q_ref,
            dst_ref=all_ref.at[me],
            send_sem=send_sem.at[step],
            recv_sem=recv_sem.at[step],
            device_id={"dp": lax.rem(me + step, n)},
            device_id_type=MESH,
        )
        copy.start()
        copies.append(copy)
    own = pltpu.make_async_copy(q_ref, all_ref.at[me], own_sem)
    own.start()
    own.wait()
    for copy in copies:
        copy.wait()


def gather_queries(queries):
    n = lax.axis_size("dp")
    return pl.pallas_call(
        gather_kernel,
        out_shape=jax.ShapeDtypeStruct((n,) + queries.shape, queries.dtype),
        in_specs=[pl.BlockSpec(memory_space=pltpu.VMEM)],
        out_specs=pl.BlockSpec(memory_space=pltpu.VMEM),
        scratch_shapes=[
            pltpu.SemaphoreType.DMA((n,)),
            pltpu.SemaphoreType.DMA((n,)),
            pltpu.SemaphoreType.DMA,
        ],
        compiler_params=pltpu.CompilerParams(collective_id=0, has_side_effects=True),
    )(queries)


def attend_kernel(
    sizes, codes, counts, totals, q_ref, k_hbm, v_hbm, acc_ref, stat_ref,
    kbuf, vbuf, kmore, vmore, ksem, vsem, moresem,
):
    rows, max_pages, span, kv_local, blocks, code_base, unroll = sizes
    q_local, head_dim = q_ref.shape[1:]
    per = 128 // span
    held = per * PRE
    b = pl.program_id(0)
    f32 = jnp.float32

    def issue(block, slot):
        @pl.loop(0, rows)
        def _(r):
            row = block * rows + r

            @pl.loop(0, jnp.minimum(counts[row], held))
            def _(s):
                page = codes[row * max_pages + s] // code_base
                pltpu.make_async_copy(k_hbm.at[page], kbuf.at[slot, r * held + s], ksem.at[slot]).start()
                pltpu.make_async_copy(v_hbm.at[page], vbuf.at[slot, r * held + s], vsem.at[slot]).start()

    @pl.when(b == 0)
    def _():
        @pl.loop(0, DEPTH)
        def _(slot):
            @pl.loop(0, rows)
            def _(r):
                vbuf[slot, pl.ds(r * held, held)] = jnp.zeros((held, span, head_dim), vbuf.dtype)

        vmore[...] = jnp.zeros(vmore.shape, vmore.dtype)
        for first in range(min(DEPTH - 1, blocks)):
            issue(first, first)

    @pl.when(b + DEPTH - 1 < blocks)
    def _():
        issue(b + DEPTH - 1, lax.rem(b + DEPTH - 1, DEPTH))

    slot = lax.rem(b, DEPTH)
    total = totals[b]
    for bit in range((rows * held).bit_length()):
        size = 1 << bit
        if size > min(rows * held, k_hbm.shape[0]):
            break

        @pl.when((total >> bit) & 1 == 1)
        def _():
            pltpu.make_async_copy(k_hbm.at[pl.ds(0, size)], kbuf.at[slot, pl.ds(0, size)], ksem.at[slot]).wait()
            pltpu.make_async_copy(v_hbm.at[pl.ds(0, size)], vbuf.at[slot, pl.ds(0, size)], vsem.at[slot]).wait()

    lane = lax.broadcasted_iota(jnp.int32, (per * q_local, 128), 1)
    line = lax.broadcasted_iota(jnp.int32, (per * q_local, 128), 0)
    fits = (lane // span == line // q_local) & (
        lane % kv_local == (line % q_local) // (q_local // kv_local)
    )
    token = jnp.where(fits, (lane % span) // kv_local, code_base)
    stat_lane = lax.broadcasted_iota(jnp.int32, (q_local, 128), 1)
    scale = head_dim ** (-0.5)

    def chunk(r, first, keys, values):
        row = b * rows + r
        scores = lax.dot_general(
            q_ref[r], keys, (((1,), (1,)), ((), ())), preferred_element_type=f32
        ) * scale
        limits = [codes[row * max_pages + first + i] % code_base for i in range(per)]
        limit = jnp.concatenate([jnp.full((q_local, 128), x, jnp.int32) for x in limits], axis=0)
        valid = token < limit
        spread = jnp.where(valid, jnp.concatenate([scores] * per, axis=0), NEG)
        peak = jnp.max(spread, axis=1, keepdims=True)
        weights = jnp.where(valid, jnp.exp(spread - peak), 0.0)
        mass = jnp.sum(weights, axis=1, keepdims=True)
        acc = jnp.dot(weights.astype(jnp.bfloat16), values, preferred_element_type=f32)
        peak = peak.reshape(per, q_local, 1)
        top = jnp.max(peak, axis=0)
        factor = jnp.exp(peak - top[None])
        mass = jnp.sum(mass.reshape(per, q_local, 1) * factor, axis=0)
        acc = jnp.sum(acc.reshape(per, q_local, head_dim) * factor, axis=0)
        return top, mass, acc

    def put_stats(r, stats, top, mass):
        return jnp.where(stat_lane == r, top, stats[0]), jnp.where(stat_lane == r, mass, stats[1])

    def first_chunk(r, stats):
        at = pl.ds(r * held, per)
        top, mass, acc = chunk(
            r, 0, kbuf[slot, at].reshape(128, head_dim), vbuf[slot, at].reshape(128, head_dim)
        )
        acc_ref[r] = acc
        return put_stats(r, stats, top, mass)

    def body(i, stats):
        for u in range(unroll):
            stats = first_chunk(i * unroll + u, stats)
        return stats

    empty = (jnp.full((q_local, 128), NEG, f32), jnp.zeros((q_local, 128), f32))
    stats = lax.fori_loop(0, rows // unroll, body, empty)
    stat_ref[0], stat_ref[1] = stats

    def merge(r, part):
        top, mass, acc = part
        here = stat_lane == r
        old_top = jnp.max(jnp.where(here, stat_ref[0], NEG), axis=1, keepdims=True)
        old_mass = jnp.sum(jnp.where(here, stat_ref[1], 0.0), axis=1, keepdims=True)
        new_top = jnp.maximum(old_top, top)
        old_f = jnp.exp(old_top - new_top)
        new_f = jnp.exp(top - new_top)
        acc_ref[r] = acc_ref[r] * old_f + acc * new_f
        stat_ref[0] = jnp.where(here, new_top, stat_ref[0])
        stat_ref[1] = jnp.where(here, old_mass * old_f + mass * new_f, stat_ref[1])

    @pl.loop(0, rows)
    def _(r):
        row = b * rows + r
        count = counts[row]

        @pl.when(count > per)
        def _():
            for j in range(1, PRE):
                at = pl.ds(r * held + j * per, per)
                merge(r, chunk(
                    r, j * per,
                    kbuf[slot, at].reshape(128, head_dim), vbuf[slot, at].reshape(128, head_dim),
                ))

            @pl.loop(PRE, jnp.maximum((count + per - 1) // per, PRE))
            def _(j):
                @pl.loop(0, jnp.minimum(count - j * per, per))
                def _(s):
                    page = codes[row * max_pages + j * per + s] // code_base
                    first = pltpu.make_async_copy(k_hbm.at[page], kmore.at[s], moresem.at[0])
                    second = pltpu.make_async_copy(v_hbm.at[page], vmore.at[s], moresem.at[1])
                    first.start()
                    second.start()
                    first.wait()
                    second.wait()

                merge(r, chunk(
                    r, j * per, kmore[...].reshape(128, head_dim), vmore[...].reshape(128, head_dim)
                ))


def attend(codes, counts, totals, all_queries, keys, values, page_len, kv_local, code_base, max_pages):
    blocks, rows, q_local, head_dim = all_queries.shape
    span = page_len * kv_local
    per = 128 // span
    held = per * PRE
    unroll = 4
    sizes = (rows, max_pages, span, kv_local, blocks, code_base, unroll)
    return pl.pallas_call(
        functools.partial(attend_kernel, sizes),
        out_shape=(
            jax.ShapeDtypeStruct((blocks, rows, q_local, head_dim), jnp.float32),
            jax.ShapeDtypeStruct((blocks, 2, q_local, 128), jnp.float32),
        ),
        grid_spec=pltpu.PrefetchScalarGridSpec(
            num_scalar_prefetch=3,
            grid=(blocks,),
            in_specs=[
                pl.BlockSpec((None, rows, q_local, head_dim), lambda b, *_: (b, 0, 0, 0)),
                pl.BlockSpec(memory_space=pl.ANY),
                pl.BlockSpec(memory_space=pl.ANY),
            ],
            out_specs=(
                pl.BlockSpec((None, rows, q_local, head_dim), lambda b, *_: (b, 0, 0, 0)),
                pl.BlockSpec((None, 2, q_local, 128), lambda b, *_: (b, 0, 0, 0)),
            ),
            scratch_shapes=[
                pltpu.VMEM((DEPTH, rows * held, span, head_dim), keys.dtype),
                pltpu.VMEM((DEPTH, rows * held, span, head_dim), keys.dtype),
                pltpu.VMEM((per, span, head_dim), keys.dtype),
                pltpu.VMEM((per, span, head_dim), keys.dtype),
                pltpu.SemaphoreType.DMA((DEPTH,)),
                pltpu.SemaphoreType.DMA((DEPTH,)),
                pltpu.SemaphoreType.DMA((2,)),
            ],
        ),
        compiler_params=pltpu.CompilerParams(dimension_semantics=("arbitrary",)),
    )(codes, counts, totals, all_queries, keys, values)


def finish_kernel(
    acc_hbm, stat_hbm, w_hbm, att_out, proj_out,
    got_acc, got_stat, weight, mixed, everyone, part, got_part,
    acc_send, acc_recv, stat_send, stat_recv, own_sem, w_sem,
    att_send, att_recv, part_send, part_recv,
):
    n = lax.axis_size("dp")
    me = lax.axis_index("dp")
    m = lax.axis_size("mp")
    mine = lax.axis_index("mp")
    rows, q_local, head_dim = att_out.shape
    out_rows = proj_out.shape[0]
    pieces = part_send.shape[1]
    width = proj_out.shape[1] // pieces
    load_w = pltpu.make_async_copy(w_hbm, weight, w_sem)
    load_w.start()
    own_acc = pltpu.make_async_copy(acc_hbm.at[me], got_acc.at[0], own_sem.at[0])
    own_stat = pltpu.make_async_copy(stat_hbm.at[me], got_stat.at[0], own_sem.at[1])
    own_acc.start()
    own_stat.start()
    axis_barrier(("dp", "mp"))

    waiting = []
    for step in range(1, n):
        peer = lax.rem(me + step, n)
        for src, dst, send, recv in (
            (stat_hbm, got_stat, stat_send, stat_recv),
            (acc_hbm, got_acc, acc_send, acc_recv),
        ):
            copy = pltpu.make_async_remote_copy(
                src_ref=src.at[peer], dst_ref=dst.at[step],
                send_sem=send.at[step], recv_sem=recv.at[step],
                device_id={"dp": peer}, device_id_type=MESH,
            )
            copy.start()
            waiting.append(copy)
    own_stat.wait()
    own_acc.wait()
    for copy in waiting:
        copy.wait()

    top = got_stat[0, 0]
    for s in range(1, n):
        top = jnp.maximum(top, got_stat[s, 0])
    factors = [jnp.exp(got_stat[s, 0] - top) for s in range(n)]
    mass = factors[0] * got_stat[0, 1]
    for s in range(1, n):
        mass = mass + factors[s] * got_stat[s, 1]
    for r in range(rows):
        total = factors[0][:, r : r + 1] * got_acc[0, r]
        for s in range(1, n):
            total = total + factors[s][:, r : r + 1] * got_acc[s, r]
        result = total / mass[:, r : r + 1]
        mixed[r] = result
        att_out[r] = result.astype(jnp.bfloat16)
    for h in range(q_local):
        everyone[me, :, h * head_dim : (h + 1) * head_dim] = mixed[:, h, :].astype(jnp.bfloat16)

    waiting = []
    for step in range(1, n):
        copy = pltpu.make_async_remote_copy(
            src_ref=everyone.at[me], dst_ref=everyone.at[me],
            send_sem=att_send.at[step], recv_sem=att_recv.at[step],
            device_id={"dp": lax.rem(me + step, n)}, device_id_type=MESH,
        )
        copy.start()
        waiting.append(copy)
    load_w.wait()
    for copy in waiting:
        copy.wait()

    waiting = []
    flat = everyone[...].reshape(n * rows, q_local * head_dim)
    for piece in range(pieces):
        value = jnp.dot(
            flat, weight[:, piece * width : (piece + 1) * width], preferred_element_type=jnp.float32
        )
        part[piece] = value.reshape(m, out_rows, width)
        for step in range(1, m):
            peer = lax.rem(mine + step, m)
            copy = pltpu.make_async_remote_copy(
                src_ref=part.at[piece, peer], dst_ref=got_part.at[piece, step],
                send_sem=part_send.at[step, piece], recv_sem=part_recv.at[step, piece],
                device_id={"mp": peer}, device_id_type=MESH,
            )
            copy.start()
            waiting.append((piece, copy))
    for piece in range(pieces):
        total = part[piece, mine]
        for at, copy in waiting:
            if at == piece:
                copy.wait()
        for step in range(1, m):
            total = total + got_part[piece, step]
        proj_out[:, piece * width : (piece + 1) * width] = total.astype(jnp.bfloat16)


def finish(acc, stat, out_weight):
    n, rows, q_local, head_dim = acc.shape
    m = lax.axis_size("mp")
    depth, columns = out_weight.shape
    out_rows = n * rows // m
    pieces = max(columns // 256, 1)
    width = columns // pieces
    dma = pltpu.SemaphoreType.DMA
    return pl.pallas_call(
        finish_kernel,
        out_shape=(
            jax.ShapeDtypeStruct((rows, q_local, head_dim), jnp.bfloat16),
            jax.ShapeDtypeStruct((out_rows, columns), jnp.bfloat16),
        ),
        in_specs=[pl.BlockSpec(memory_space=pl.ANY)] * 3,
        out_specs=(pl.BlockSpec(memory_space=pltpu.VMEM),) * 2,
        scratch_shapes=[
            pltpu.VMEM((n, rows, q_local, head_dim), jnp.float32),
            pltpu.VMEM((n, 2, q_local, 128), jnp.float32),
            pltpu.VMEM((depth, columns), out_weight.dtype),
            pltpu.VMEM((rows, q_local, head_dim), jnp.float32),
            pltpu.VMEM((n, rows, q_local * head_dim), jnp.bfloat16),
            pltpu.VMEM((pieces, m, out_rows, width), jnp.float32),
            pltpu.VMEM((pieces, m, out_rows, width), jnp.float32),
            dma((n,)), dma((n,)), dma((n,)), dma((n,)), dma((2,)), dma,
            dma((n,)), dma((n,)), dma((m, pieces)), dma((m, pieces)),
        ],
        compiler_params=pltpu.CompilerParams(collective_id=1, has_side_effects=True),
    )(acc, stat, out_weight)


def shards(queries, lookup_sheets, content_sheets, page_table, context_len, out_weight):
    req_rows, max_pages = page_table.shape
    pool_local, page_len, kv_local, head_dim = lookup_sheets.shape
    dp_count = lax.axis_size("dp")
    rows_mine = req_rows // dp_count
    code_base = 2 * page_len
    span = page_len * kv_local
    held = (128 // span) * PRE

    local = page_table - lax.axis_index("dp") * pool_local
    slots = jnp.arange(max_pages, dtype=jnp.int32)
    used = jnp.clip(context_len[:, None] - slots[None, :] * page_len, 0, page_len)
    wanted = (local >= 0) & (local < pool_local) & (used > 0)
    before = (slots[:, None] < slots[None, :]).astype(jnp.bfloat16)
    rank = jnp.dot(
        wanted.astype(jnp.bfloat16), before, preferred_element_type=jnp.float32
    ).astype(jnp.int32)
    code = jnp.where(wanted, local * code_base + used, 0)
    rank = jnp.where(wanted, rank, -1)
    codes = jnp.sum(
        jnp.where(rank[:, None, :] == slots[None, :, None], code[:, None, :], 0), axis=2
    )
    counts = jnp.sum(wanted.astype(jnp.int32), axis=1)
    totals = jnp.sum(jnp.minimum(counts, held).reshape(dp_count, rows_mine), axis=1)

    all_queries = gather_queries(queries)
    acc, stat = attend(
        codes.reshape(-1), counts, totals, all_queries,
        lookup_sheets.reshape(pool_local, span, head_dim),
        content_sheets.reshape(pool_local, span, head_dim),
        page_len, kv_local, code_base, max_pages,
    )
    return finish(acc, stat, out_weight)


def solution(mesh):
    placed = (
        P("dp", "mp", None),
        P("dp", None, "mp", None),
        P("dp", None, "mp", None),
        P(),
        P(),
        P("mp", "dp"),
    )
    return jax.shard_map(
        shards,
        mesh=mesh,
        in_specs=placed,
        out_specs=(P("dp", "mp", None), P("mp", "dp")),
        check_vma=False,
    )
```

time: 335 us -> 220 us (0.66)
  the two profiles are of different devices: /device:TPU:0 before, /device:TPU:21 now
where the time goes in v1:
time: 220 us; the launch traced here: 219 us
  Pallas kernels  212 us (96%)
  local copies, waits for them, and re-layouts  4.02 us (2%)
  other arithmetic  2.52 us (1%)
    pallas_call x1, Pallas kernels, finish(): pl.pallas_call(finish_kernel, out_shape=(jax.ShapeDtypeStruct((rows, q_lo...  98.8 us
    pallas_call x1, Pallas kernels, attend(): pl.pallas_call(functools.partial(attend_kernel, sizes), out_shape=(jax.Sh...  87.2 us
    pallas_call x1, Pallas kernels, gather_queries(): pl.pallas_call(gather_kernel, out_shape=jax.ShapeDtypeStruct((n,) + queri...  25.8 us

profile of v1, /device:TPU:21, one launch (start us, length us, event | category | flops | bytes accessed | tf_op | source)
XLA Modules:
  0.0 219.2 jit_solution(16243475639203118951)
XLA Ops:
  0.6 0.9 convert_reduce_fusion
  1.5 0.0 copy-start
  1.5 0.1 min.22
  1.6 0.6 reduce_sum.29.totals
  2.3 0.8 add_select_fusion
  3.1 0.2 fusion
  3.3 0.2 select_reduce_fusion
  3.5 0.1 copy.12
  3.6 0.7 reshape.25.codes
  4.3 25.8 %shard_map.77.q_ref = bf16[8,32,16,128]{3,2,1,0:T(8,128)(2,1)} custom-call(bf16[32,16,128]{2,1,0:T(8,128)(2,1)} %q_ref.1), custom_call_target="tpu_custom_call" | custom-call | tf_op jit(solution)/shard_map/pallas_call | solution.py:55
  30.1 0.0 copy-done
  30.1 87.2 %shard_map.78 = (f32[8,32,16,128]{3,2,1,0:T(8,128)}, f32[8,2,16,128]{3,2,1,0:T(8,128)}) custom-call(s32[8192]{0:T(1024)} %reshape.25.codes, s32[256]{0:T(256)} %copy-done, s32[8]{0:T(128)} %reduce_sum.29.totals, bf16[8,32,16,128]{3,2,1,0:T(8,128)(2,1)} %shard_map.77.q_ref, bf16[1024,32,128]{2,1,0:T(8,128)(2,1)} %bitcast.3, bf16[1024,32,128]{2,1,0:T(8,128)(2,1)} %bitcast.4), custom_call_target="tpu_custom_call" | custom-call | tf_op jit(solution)/shard_map/pallas_call | solution.py:218
  117.3 98.8 %shard_map.79 = (bf16[32,16,128]{2,1,0:T(8,128)(2,1)}, bf16[64,1024]{1,0:T(8,128)(2,1)}) custom-call(f32[8,32,16,128]{3,2,1,0:T(8,128)} %get-tuple-element.4.acc_hbm, f32[8,2,16,128]{3,2,1,0:T(8,128)} %get-tuple-element.5.stat_hbm, bf16[2048,1024]{1,0:T(8,128)(2,1)} %w_hbm.1), custom_call_target="tpu_custom_call" | custom-call | tf_op jit(solution)/shard_map/pallas_call | solution.py:355
  216.1 1.6 copy.19
  217.7 1.6 copy.20
  (2 shorter events, 0.0 us)
Async XLA Ops:
  1.5 28.5 %copy-start = (s32[256]{0:T(256)}, s32[256]{0:T(256)S(1)}, u32[]{:S(2)}) copy-start(s32[256]{0:T(256)S(1)} %get-tuple-element.6.counts) | copy-start | bytes 3076

commit v2 on v1

--- a/solution.py
+++ b/solution.py
@@ -27,27 +27,83 @@
     pl.semaphore_wait(barrier, total)
 
 
-def gather_kernel(q_ref, all_ref, send_sem, recv_sem, own_sem):
+def line_gather(buf, right_sem, left_sem, side_sem, recv_sem):
     n = lax.axis_size("dp")
     me = lax.axis_index("dp")
+    length = n // 2
+    spot = me // 2
+    side = lax.rem(me, 2)
+
+    def send(piece, sem, target):
+        return pltpu.make_async_remote_copy(
+            src_ref=buf.at[piece], dst_ref=buf.at[piece],
+            send_sem=sem, recv_sem=recv_sem.at[piece],
+            device_id={"dp": target}, device_id_type=MESH,
+        )
+
+    def arrive(piece):
+        send(piece, side_sem.at[0], me).wait_recv()
+
+    def to_right(t):
+        return send((spot - t) * 2 + side, right_sem.at[t], me + 2)
+
+    def to_left(t):
+        return send((spot + t) * 2 + side, left_sem.at[t], me - 2)
+
+    def across(at):
+        return send(at * 2 + side, side_sem.at[at], spot * 2 + 1 - side)
+
+    has_right = spot < length - 1
+    has_left = spot > 0
+    for t in range(length):
+        @pl.when(spot - t >= 0)
+        def _():
+            if t:
+                arrive((spot - t) * 2 + side)
+
+            @pl.when(has_right)
+            def _():
+                to_right(t).start()
+
+            if t:
+                across(spot - t).start()
+
+        @pl.when(spot + t < length)
+        def _():
+            if t:
+                arrive((spot + t) * 2 + side)
+
+            @pl.when(has_left)
+            def _():
+                to_left(t).start()
+
+            across(spot + t).start()
+
+    for at in range(length):
+        arrive(at * 2 + 1 - side)
+        across(at).wait_send()
+    for t in range(length):
+        @pl.when((spot - t >= 0) & has_right)
+        def _():
+            to_right(t).wait_send()
+
+        @pl.when((spot + t < length) & has_left)
+        def _():
+            to_left(t).wait_send()
+
+
+def line_sems():
+    n = lax.axis_size("dp")
+    dma = pltpu.SemaphoreType.DMA
+    return [dma((n // 2,)), dma((n // 2,)), dma((n // 2,)), dma((n,))]
+
+
+def gather_kernel(q_ref, all_ref, own_sem, *sems):
+    own = pltpu.make_async_copy(q_ref, all_ref.at[lax.axis_index("dp")], own_sem)
+    own.start()
     axis_barrier(("dp",))
-    copies = []
-    for step in range(1, n):
-        copy = pltpu.make_async_remote_copy(
-            src_ref=q_ref,
-            dst_ref=all_ref.at[me],
-            send_sem=send_sem.at[step],
-            recv_sem=recv_sem.at[step],
-            device_id={"dp": lax.rem(me + step, n)},
-            device_id_type=MESH,
-        )
-        copy.start()
-        copies.append(copy)
-    own = pltpu.make_async_copy(q_ref, all_ref.at[me], own_sem)
-    own.start()
     own.wait()
-    for copy in copies:
-        copy.wait()
+    line_gather(all_ref, *sems)
 
 
 def gather_queries(queries):
@@ -57,18 +113,14 @@
         out_shape=jax.ShapeDtypeStruct((n,) + queries.shape, queries.dtype),
         in_specs=[pl.BlockSpec(memory_space=pltpu.VMEM)],
         out_specs=pl.BlockSpec(memory_space=pltpu.VMEM),
-        scratch_shapes=[
-            pltpu.SemaphoreType.DMA((n,)),
-            pltpu.SemaphoreType.DMA((n,)),
-            pltpu.SemaphoreType.DMA,
-        ],
+        scratch_shapes=[pltpu.SemaphoreType.DMA] + line_sems(),
         compiler_params=pltpu.CompilerParams(collective_id=0, has_side_effects=True),
     )(queries)
 
 
 def attend_kernel(
-    sizes, codes, counts, totals, q_ref, k_hbm, v_hbm, acc_ref, stat_ref,
-    kbuf, vbuf, kmore, vmore, ksem, vsem, moresem,
+    sizes, codes, counts, totals, q_ref, k_hbm, v_hbm, code_ref, stat_ref,
+    acc_ref, kbuf, vbuf, kmore, vmore, ksem, vsem, moresem,
 ):
     rows, max_pages, span, kv_local, blocks, code_base, unroll = sizes
     q_local, head_dim = q_ref.shape[1:]
@@ -84,7 +136,7 @@
 
             @pl.loop(0, jnp.minimum(counts[row], held))
             def _(s):
-                page = codes[row * max_pages + s] // code_base
+                page = lax.div(codes[row * max_pages + s], code_base)
                 pltpu.make_async_copy(k_hbm.at[page], kbuf.at[slot, r * held + s], ksem.at[slot]).start()
                 pltpu.make_async_copy(v_hbm.at[page], vbuf.at[slot, r * held + s], vsem.at[slot]).start()
 
@@ -125,12 +177,14 @@
     stat_lane = lax.broadcasted_iota(jnp.int32, (q_local, 128), 1)
     scale = head_dim ** (-0.5)
 
-    def chunk(r, first, keys, values):
-        row = b * rows + r
-        scores = lax.dot_general(
+    def raw_scores(r, keys):
+        return lax.dot_general(
             q_ref[r], keys, (((1,), (1,)), ((), ())), preferred_element_type=f32
         ) * scale
-        limits = [codes[row * max_pages + first + i] % code_base for i in range(per)]
+
+    def chunk(r, first, scores, values):
+        row = b * rows + r
+        limits = [lax.rem(codes[row * max_pages + first + i], code_base) for i in range(per)]
         limit = jnp.concatenate([jnp.full((q_local, 128), x, jnp.int32) for x in limits], axis=0)
         valid = token < limit
         spread = jnp.where(valid, jnp.concatenate([scores] * per, axis=0), NEG)
@@ -151,7 +205,7 @@
     def first_chunk(r, stats):
         at = pl.ds(r * held, per)
         top, mass, acc = chunk(
-            r, 0, kbuf[slot, at].reshape(128, head_dim), vbuf[slot, at].reshape(128, head_dim)
+            r, 0, acc_ref[r], vbuf[slot, at].reshape(128, head_dim)
         )
         acc_ref[r] = acc
         return put_stats(r, stats, top, mass)
@@ -160,6 +214,12 @@
         for u in range(unroll):
             stats = first_chunk(i * unroll + u, stats)
         return stats
+
+    @pl.loop(0, rows // unroll)
+    def _(i):
+        for u in range(unroll):
+            r = i * unroll + u
+            acc_ref[r] = raw_scores(r, kbuf[slot, pl.ds(r * held, per)].reshape(128, head_dim))
 
     empty = (jnp.full((q_local, 128), NEG, f32), jnp.zeros((q_local, 128), f32))
     stats = lax.fori_loop(0, rows // unroll, body, empty)
@@ -188,14 +248,15 @@
                 at = pl.ds(r * held + j * per, per)
                 merge(r, chunk(
                     r, j * per,
-                    kbuf[slot, at].reshape(128, head_dim), vbuf[slot, at].reshape(128, head_dim),
+                    raw_scores(r, kbuf[slot, at].reshape(128, head_dim)),
+                    vbuf[slot, at].reshape(128, head_dim),
                 ))
 
             @pl.loop(PRE, jnp.maximum((count + per - 1) // per, PRE))
             def _(j):
                 @pl.loop(0, jnp.minimum(count - j * per, per))
                 def _(s):
-                    page = codes[row * max_pages + j * per + s] // code_base
+                    page = lax.div(codes[row * max_pages + j * per + s], code_base)
                     first = pltpu.make_async_copy(k_hbm.at[page], kmore.at[s], moresem.at[0])
                     second = pltpu.make_async_copy(v_hbm.at[page], vmore.at[s], moresem.at[1])
                     first.start()
@@ -204,8 +265,21 @@
                     second.wait()
 
                 merge(r, chunk(
-                    r, j * per, kmore[...].reshape(128, head_dim), vmore[...].reshape(128, head_dim)
+                    r, j * per, raw_scores(r, kmore[...].reshape(128, head_dim)),
+                    vmore[...].reshape(128, head_dim),
                 ))
+
+    def encode(i, steps):
+        for u in range(unroll):
+            r = i * unroll + u
+            acc = acc_ref[r]
+            step = jnp.max(jnp.abs(acc), axis=1, keepdims=True) * (1.0 / 32767.0)
+            inverse = jnp.where(step > 1e-30, 1.0 / jnp.maximum(step, 1e-30), 0.0)
+            code_ref[r] = jnp.round(acc * inverse).astype(jnp.int32).astype(jnp.int16)
+            steps = jnp.where(stat_lane == r, step, steps)
+        return steps
+
+    stat_ref[2] = lax.fori_loop(0, rows // unroll, encode, jnp.zeros((q_local, 128), f32))
 
 
 def attend(codes, counts, totals, all_queries, keys, values, page_len, kv_local, code_base, max_pages):
@@ -213,13 +287,13 @@
     span = page_len * kv_local
     per = 128 // span
     held = per * PRE
-    unroll = 4
+    unroll = 16 if rows % 16 == 0 else 1
     sizes = (rows, max_pages, span, kv_local, blocks, code_base, unroll)
     return pl.pallas_call(
         functools.partial(attend_kernel, sizes),
         out_shape=(
-            jax.ShapeDtypeStruct((blocks, rows, q_local, head_dim), jnp.float32),
-            jax.ShapeDtypeStruct((blocks, 2, q_local, 128), jnp.float32),
+            jax.ShapeDtypeStruct((blocks, rows, q_local, head_dim), jnp.int16),
+            jax.ShapeDtypeStruct((blocks, 3, q_local, 128), jnp.float32),
         ),
         grid_spec=pltpu.PrefetchScalarGridSpec(
             num_scalar_prefetch=3,
@@ -231,9 +305,10 @@
             ],
             out_specs=(
                 pl.BlockSpec((None, rows, q_local, head_dim), lambda b, *_: (b, 0, 0, 0)),
-                pl.BlockSpec((None, 2, q_local, 128), lambda b, *_: (b, 0, 0, 0)),
+                pl.BlockSpec((None, 3, q_local, 128), lambda b, *_: (b, 0, 0, 0)),
             ),
             scratch_shapes=[
+                pltpu.VMEM((rows, q_local, head_dim), jnp.float32),
                 pltpu.VMEM((DEPTH, rows * held, span, head_dim), keys.dtype),
                 pltpu.VMEM((DEPTH, rows * held, span, head_dim), keys.dtype),
                 pltpu.VMEM((per, span, head_dim), keys.dtype),
@@ -249,9 +324,10 @@
 
 def finish_kernel(
     acc_hbm, stat_hbm, w_hbm, att_out, proj_out,
-    got_acc, got_stat, weight, mixed, everyone, part, got_part,
+    got_acc, got_stat, weight, mixed, everyone, part, got_pair, summed, got_part,
     acc_send, acc_recv, stat_send, stat_recv, own_sem, w_sem,
-    att_send, att_recv, part_send, part_recv,
+    pair_send, pair_recv, part_send, part_recv,
+    right_sem, left_sem, side_sem, line_recv,
 ):
     n = lax.axis_size("dp")
     me = lax.axis_index("dp")
@@ -259,7 +335,7 @@
     mine = lax.axis_index("mp")
     rows, q_local, head_dim = att_out.shape
     out_rows = proj_out.shape[0]
-    pieces = part_send.shape[1]
+    pieces = pair_send.shape[0]
     width = proj_out.shape[1] // pieces
     load_w = pltpu.make_async_copy(w_hbm, weight, w_sem)
     load_w.start()
@@ -295,51 +371,55 @@
     mass = factors[0] * got_stat[0, 1]
     for s in range(1, n):
         mass = mass + factors[s] * got_stat[s, 1]
+    gains = [factors[s] * got_stat[s, 2] / mass for s in range(n)]
     for r in range(rows):
-        total = factors[0][:, r : r + 1] * got_acc[0, r]
+        result = gains[0][:, r : r + 1] * got_acc[0, r].astype(jnp.float32)
         for s in range(1, n):
-            total = total + factors[s][:, r : r + 1] * got_acc[s, r]
-        result = total / mass[:, r : r + 1]
+            result = result + gains[s][:, r : r + 1] * got_acc[s, r].astype(jnp.float32)
         mixed[r] = result
         att_out[r] = result.astype(jnp.bfloat16)
     for h in range(q_local):
         everyone[me, :, h * head_dim : (h + 1) * head_dim] = mixed[:, h, :].astype(jnp.bfloat16)
 
-    waiting = []
-    for step in range(1, n):
-        copy = pltpu.make_async_remote_copy(
-            src_ref=everyone.at[me], dst_ref=everyone.at[me],
-            send_sem=att_send.at[step], recv_sem=att_recv.at[step],
-            device_id={"dp": lax.rem(me + step, n)}, device_id_type=MESH,
+    line_gather(everyone, right_sem, left_sem, side_sem, line_recv)
+    load_w.wait()
+
+    pair = lax.rem(mine, 2)
+    group = mine // 2
+    groups = m // 2
+
+    def pair_copy(piece):
+        return pltpu.make_async_remote_copy(
+            src_ref=part.at[piece, :, 1 - pair], dst_ref=got_pair.at[piece],
+            send_sem=pair_send.at[piece], recv_sem=pair_recv.at[piece],
+            device_id={"mp": group * 2 + 1 - pair}, device_id_type=MESH,
         )
-        copy.start()
-        waiting.append(copy)
-    load_w.wait()
-    for copy in waiting:
-        copy.wait()
-
-    waiting = []
+
+    def group_copy(piece, step):
+        return pltpu.make_async_remote_copy(
+            src_ref=summed.at[piece, step], dst_ref=got_part.at[piece, step],
+            send_sem=part_send.at[step, piece], recv_sem=part_recv.at[step, piece],
+            device_id={"mp": lax.rem(group + step, groups) * 2 + pair}, device_id_type=MESH,
+        )
+
     flat = everyone[...].reshape(n * rows, q_local * head_dim)
     for piece in range(pieces):
         value = jnp.dot(
             flat, weight[:, piece * width : (piece + 1) * width], preferred_element_type=jnp.float32
         )
-        part[piece] = value.reshape(m, out_rows, width)
-        for step in range(1, m):
-            peer = lax.rem(mine + step, m)
-            copy = pltpu.make_async_remote_copy(
-                src_ref=part.at[piece, peer], dst_ref=got_part.at[piece, step],
-                send_sem=part_send.at[step, piece], recv_sem=part_recv.at[step, piece],
-                device_id={"mp": peer}, device_id_type=MESH,
-            )
-            copy.start()
-            waiting.append((piece, copy))
+        part[piece] = value.reshape(groups, 2, out_rows, width)
+        pair_copy(piece).start()
     for piece in range(pieces):
-        total = part[piece, mine]
-        for at, copy in waiting:
-            if at == piece:
-                copy.wait()
-        for step in range(1, m):
+        pair_copy(piece).wait()
+        for step in range(groups):
+            at = lax.rem(group + step, groups)
+            summed[piece, step] = part[piece, at, pair] + got_pair[piece, at]
+        for step in range(1, groups):
+            group_copy(piece, step).start()
+    for piece in range(pieces):
+        total = summed[piece, 0]
+        for step in range(1, groups):
+            group_copy(piece, step).wait()
             total = total + got_part[piece, step]
         proj_out[:, piece * width : (piece + 1) * width] = total.astype(jnp.bfloat16)
 
@@ -361,16 +441,18 @@
         in_specs=[pl.BlockSpec(memory_space=pl.ANY)] * 3,
         out_specs=(pl.BlockSpec(memory_space=pltpu.VMEM),) * 2,
         scratch_shapes=[
-            pltpu.VMEM((n, rows, q_local, head_dim), jnp.float32),
-            pltpu.VMEM((n, 2, q_local, 128), jnp.float32),
+            pltpu.VMEM((n, rows, q_local, head_dim), acc.dtype),
+            pltpu.VMEM((n, 3, q_local, 128), jnp.float32),
             pltpu.VMEM((depth, columns), out_weight.dtype),
             pltpu.VMEM((rows, q_local, head_dim), jnp.float32),
             pltpu.VMEM((n, rows, q_local * head_dim), jnp.bfloat16),
-            pltpu.VMEM((pieces, m, out_rows, width), jnp.float32),
-            pltpu.VMEM((pieces, m, out_rows, width), jnp.float32),
+            pltpu.VMEM((pieces, m // 2, 2, out_rows, width), jnp.float32),
+            pltpu.VMEM((pieces, m // 2, out_rows, width), jnp.float32),
+            pltpu.VMEM((pieces, m // 2, out_rows, width), jnp.float32),
+            pltpu.VMEM((pieces, m // 2, out_rows, width), jnp.float32),
             dma((n,)), dma((n,)), dma((n,)), dma((n,)), dma((2,)), dma,
-            dma((n,)), dma((n,)), dma((m, pieces)), dma((m, pieces)),
-        ],
+            dma((pieces,)), dma((pieces,)), dma((m // 2, pieces)), dma((m // 2, pieces)),
+        ] + line_sems(),
         compiler_params=pltpu.CompilerParams(collective_id=1, has_side_effects=True),
     )(acc, stat, out_weight)
 

time: 220 us -> 128 us (0.58)
  the two profiles are of different devices: /device:TPU:21 before, /device:TPU:0 now
where the time goes in v2:
time: 128 us; the launch traced here: 129 us
  Pallas kernels  121 us (95%)
  local copies, waits for them, and re-layouts  4.03 us (3%)
  other arithmetic  2.57 us (2%)
    pallas_call x1, Pallas kernels, finish(): pl.pallas_call(finish_kernel, out_shape=(jax.ShapeDtypeStruct((rows, q_lo...  63.2 us
    pallas_call x1, Pallas kernels, attend(): pl.pallas_call(functools.partial(attend_kernel, sizes), out_shape=(jax.Sh...  34.2 us
    pallas_call x1, Pallas kernels, gather_queries(): pl.pallas_call(gather_kernel, out_shape=jax.ShapeDtypeStruct((n,) + queri...  23.5 us
    unnamed x4, local copies, waits for them, and re-layouts  3.14 us

profile of v2, /device:TPU:0, one launch (start us, length us, event | category | flops | bytes accessed | tf_op | source)
XLA Modules:
  0.0 128.5 jit_solution(13550381624321514715)
XLA Ops:
  0.6 0.9 convert_reduce_fusion
  1.5 0.0 copy-start
  1.5 0.1 min.22
  1.6 0.7 reduce_sum.29.totals
  2.3 0.8 add_select_fusion
  3.2 0.2 fusion
  3.4 0.2 select_reduce_fusion
  3.5 0.1 copy.12
  3.6 0.7 reshape.25.codes
  4.3 23.5 %shard_map.77.q_ref = bf16[8,32,16,128]{3,2,1,0:T(8,128)(2,1)} custom-call(bf16[32,16,128]{2,1,0:T(8,128)(2,1)} %q_ref.1), custom_call_target="tpu_custom_call" | custom-call | tf_op jit(solution)/shard_map/pallas_call | solution.py:111
  27.9 0.0 copy-done
  27.9 34.2 %shard_map.78 = (s16[8,32,16,128]{3,2,1,0:T(8,128)(2,1)}, f32[8,3,16,128]{3,2,1,0:T(8,128)}) custom-call(s32[8192]{0:T(1024)} %reshape.25.codes, s32[256]{0:T(256)} %copy-done, s32[8]{0:T(128)} %reduce_sum.29.totals, bf16[8,32,16,128]{3,2,1,0:T(8,128)(2,1)} %shard_map.77.q_ref, bf16[1024,32,128]{2,1,0:T(8,128)(2,1)} %bitcast.3, bf16[1024,32,128]{2,1,0:T(8,128)(2,1)} %bitcast.4), custom_call_target="tpu_custom_call" | custom-call | tf_op jit(solution)/shard_map/pallas_call | solution.py:292
  62.1 63.2 %shard_map.79 = (bf16[32,16,128]{2,1,0:T(8,128)(2,1)}, bf16[64,1024]{1,0:T(8,128)(2,1)}) custom-call(s16[8,32,16,128]{3,2,1,0:T(8,128)(2,1)} %get-tuple-element.4.acc_hbm, f32[8,3,16,128]{3,2,1,0:T(8,128)} %get-tuple-element.5.stat_hbm, bf16[2048,1024]{1,0:T(8,128)(2,1)} %w_hbm.1), custom_call_target="tpu_custom_call" | custom-call | tf_op jit(solution)/shard_map/pallas_call | solution.py:435
  125.4 1.6 %copy.19 = bf16[32,16,128]{2,1,0:T(8,128)(2,1)} copy(bf16[32,16,128]{2,1,0:T(8,128)(2,1)} %get-tuple-element.10) | data formatting | bytes 262144
  126.9 1.6 %copy.20 = bf16[64,1024]{1,0:T(8,128)(2,1)} copy(bf16[64,1024]{1,0:T(8,128)(2,1)} %get-tuple-element.11) | data formatting | bytes 262144
  (2 shorter events, 0.0 us)
Async XLA Ops:
  1.5 26.4 %copy-start = (s32[256]{0:T(256)}, s32[256]{0:T(256)S(1)}, u32[]{:S(2)}) copy-start(s32[256]{0:T(256)S(1)} %get-tuple-element.6.counts) | copy-start | bytes 3076

commit v3 on v2

--- a/solution.py
+++ b/solution.py
@@ -274,7 +274,9 @@
             r = i * unroll + u
             acc = acc_ref[r]
             step = jnp.max(jnp.abs(acc), axis=1, keepdims=True) * (1.0 / 32767.0)
-            inverse = jnp.where(step > 1e-30, 1.0 / jnp.maximum(step, 1e-30), 0.0)
+            floor = jnp.maximum(step, 1e-30)
+            inverse = 1.0 / floor
+            inverse = jnp.where(step > 1e-30, inverse * (2.0 - floor * inverse), 0.0)
             code_ref[r] = jnp.round(acc * inverse).astype(jnp.int32).astype(jnp.int16)
             steps = jnp.where(stat_lane == r, step, steps)
         return steps
@@ -287,7 +289,7 @@
     span = page_len * kv_local
     per = 128 // span
     held = per * PRE
-    unroll = 16 if rows % 16 == 0 else 1
+    unroll = 32 if rows % 32 == 0 else 1
     sizes = (rows, max_pages, span, kv_local, blocks, code_base, unroll)
     return pl.pallas_call(
         functools.partial(attend_kernel, sizes),
@@ -345,23 +347,23 @@
     own_stat.start()
     axis_barrier(("dp", "mp"))
 
-    waiting = []
+    stat_copies, acc_copies = [None], [None]
     for step in range(1, n):
         peer = lax.rem(me + step, n)
-        for src, dst, send, recv in (
-            (stat_hbm, got_stat, stat_send, stat_recv),
-            (acc_hbm, got_acc, acc_send, acc_recv),
+        for src, dst, send, recv, copies in (
+            (stat_hbm, got_stat, stat_send, stat_recv, stat_copies),
+            (acc_hbm, got_acc, acc_send, acc_recv, acc_copies),
         ):
-            copy = pltpu.make_async_remote_copy(
+            copies.append(pltpu.make_async_remote_copy(
                 src_ref=src.at[peer], dst_ref=dst.at[step],
                 send_sem=send.at[step], recv_sem=recv.at[step],
                 device_id={"dp": peer}, device_id_type=MESH,
-            )
+            ))
+    for copies in (stat_copies, acc_copies):
+        for copy in copies[1:]:
             copy.start()
-            waiting.append(copy)
     own_stat.wait()
-    own_acc.wait()
-    for copy in waiting:
+    for copy in stat_copies[1:]:
         copy.wait()
 
     top = got_stat[0, 0]
@@ -372,12 +374,14 @@
     for s in range(1, n):
         mass = mass + factors[s] * got_stat[s, 1]
     gains = [factors[s] * got_stat[s, 2] / mass for s in range(n)]
-    for r in range(rows):
-        result = gains[0][:, r : r + 1] * got_acc[0, r].astype(jnp.float32)
-        for s in range(1, n):
-            result = result + gains[s][:, r : r + 1] * got_acc[s, r].astype(jnp.float32)
-        mixed[r] = result
-        att_out[r] = result.astype(jnp.bfloat16)
+    own_acc.wait()
+    for s in range(n):
+        if s:
+            acc_copies[s].wait()
+        for r in range(rows):
+            term = gains[s][:, r : r + 1] * got_acc[s, r].astype(jnp.float32)
+            mixed[r] = mixed[r] + term if s else term
+    att_out[...] = mixed[...].astype(jnp.bfloat16)
     for h in range(q_local):
         everyone[me, :, h * head_dim : (h + 1) * head_dim] = mixed[:, h, :].astype(jnp.bfloat16)
 

time: 128 us -> 121 us (0.945); the launches traced: 129 us -> 120 us
  Pallas kernels: 121 us -> 112 us
    pallas_call x1, Pallas kernels: 34.2 us -> 28.6 us  [attend(): pl.pallas_call(functools.partial(attend_kernel, sizes), out_shape=(jax.Sh...]
    pallas_call x1, Pallas kernels: 63.2 us -> 60.2 us  [finish(): pl.pallas_call(finish_kernel, out_shape=(jax.ShapeDtypeStruct((rows, q_lo...]
where the time goes in v3:
time: 121 us; the launch traced here: 120 us
  Pallas kernels  112 us (93%)
  local copies, waits for them, and re-layouts  4.03 us (3%)
  other arithmetic  2.57 us (2%)
    pallas_call x1, Pallas kernels, finish(): pl.pallas_call(finish_kernel, out_shape=(jax.ShapeDtypeStruct((rows, q_lo...  60.2 us
    pallas_call x1, Pallas kernels, attend(): pl.pallas_call(functools.partial(attend_kernel, sizes), out_shape=(jax.Sh...  28.6 us
    pallas_call x1, Pallas kernels, gather_queries(): pl.pallas_call(gather_kernel, out_shape=jax.ShapeDtypeStruct((n,) + queri...  23.5 us
    unnamed x4, local copies, waits for them, and re-layouts  3.14 us

profile of v3, /device:TPU:0, one launch (start us, length us, event | category | flops | bytes accessed | tf_op | source)
XLA Modules:
  0.0 119.9 jit_solution(15621858416250273791)
XLA Ops:
  0.6 0.9 convert_reduce_fusion
  1.5 0.0 copy-start
  1.5 0.1 min.22
  1.6 0.7 reduce_sum.29.totals
  2.3 0.8 add_select_fusion
  3.2 0.2 fusion
  3.4 0.2 select_reduce_fusion
  3.5 0.1 copy.12
  3.6 0.7 reshape.25.codes
  4.3 23.5 %shard_map.77.q_ref = bf16[8,32,16,128]{3,2,1,0:T(8,128)(2,1)} custom-call(bf16[32,16,128]{2,1,0:T(8,128)(2,1)} %q_ref.1), custom_call_target="tpu_custom_call" | custom-call | tf_op jit(solution)/shard_map/pallas_call | solution.py:111
  27.9 0.0 copy-done
  27.9 28.6 %shard_map.78 = (s16[8,32,16,128]{3,2,1,0:T(8,128)(2,1)}, f32[8,3,16,128]{3,2,1,0:T(8,128)}) custom-call(s32[8192]{0:T(1024)} %reshape.25.codes, s32[256]{0:T(256)} %copy-done, s32[8]{0:T(128)} %reduce_sum.29.totals, bf16[8,32,16,128]{3,2,1,0:T(8,128)(2,1)} %shard_map.77.q_ref, bf16[1024,32,128]{2,1,0:T(8,128)(2,1)} %bitcast.3, bf16[1024,32,128]{2,1,0:T(8,128)(2,1)} %bitcast.4), custom_call_target="tpu_custom_call" | custom-call | tf_op jit(solution)/shard_map/pallas_call | solution.py:294
  56.5 60.2 %shard_map.79 = (bf16[32,16,128]{2,1,0:T(8,128)(2,1)}, bf16[64,1024]{1,0:T(8,128)(2,1)}) custom-call(s16[8,32,16,128]{3,2,1,0:T(8,128)(2,1)} %get-tuple-element.4.acc_hbm, f32[8,3,16,128]{3,2,1,0:T(8,128)} %get-tuple-element.5.stat_hbm, bf16[2048,1024]{1,0:T(8,128)(2,1)} %w_hbm.1), custom_call_target="tpu_custom_call" | custom-call | tf_op jit(solution)/shard_map/pallas_call | solution.py:439
  116.8 1.6 %copy.19 = bf16[32,16,128]{2,1,0:T(8,128)(2,1)} copy(bf16[32,16,128]{2,1,0:T(8,128)(2,1)} %get-tuple-element.10) | data formatting | bytes 262144
  118.3 1.6 %copy.20 = bf16[64,1024]{1,0:T(8,128)(2,1)} copy(bf16[64,1024]{1,0:T(8,128)(2,1)} %get-tuple-element.11) | data formatting | bytes 262144
  (2 shorter events, 0.0 us)
Async XLA Ops:
  1.5 26.4 %copy-start = (s32[256]{0:T(256)}, s32[256]{0:T(256)S(1)}, u32[]{:S(2)}) copy-start(s32[256]{0:T(256)S(1)} %get-tuple-element.6.counts) | copy-start | bytes 3076

commit v4 on v3

--- a/solution.py
+++ b/solution.py
@@ -11,6 +11,7 @@
 NEG = -1e30
 DEPTH = 4
 PRE = 2
+PARTS = 2
 
 
 def axis_barrier(axes):
@@ -34,68 +35,72 @@
     spot = me // 2
     side = lax.rem(me, 2)
 
-    def send(piece, sem, target):
+    half = buf.shape[1] // PARTS
+
+    def send(piece, h, sem, target):
+        at = buf.at[piece, pl.ds(h * half, half)]
         return pltpu.make_async_remote_copy(
-            src_ref=buf.at[piece], dst_ref=buf.at[piece],
-            send_sem=sem, recv_sem=recv_sem.at[piece],
+            src_ref=at, dst_ref=at, send_sem=sem, recv_sem=recv_sem.at[piece, h],
             device_id={"dp": target}, device_id_type=MESH,
         )
 
-    def arrive(piece):
-        send(piece, side_sem.at[0], me).wait_recv()
-
-    def to_right(t):
-        return send((spot - t) * 2 + side, right_sem.at[t], me + 2)
-
-    def to_left(t):
-        return send((spot + t) * 2 + side, left_sem.at[t], me - 2)
-
-    def across(at):
-        return send(at * 2 + side, side_sem.at[at], spot * 2 + 1 - side)
+    def arrive(piece, h):
+        send(piece, h, side_sem.at[0, h], me).wait_recv()
+
+    def to_right(t, h):
+        return send((spot - t) * 2 + side, h, right_sem.at[t, h], me + 2)
+
+    def to_left(t, h):
+        return send((spot + t) * 2 + side, h, left_sem.at[t, h], me - 2)
+
+    def across(at, h):
+        return send(at * 2 + side, h, side_sem.at[at, h], spot * 2 + 1 - side)
 
     has_right = spot < length - 1
     has_left = spot > 0
     for t in range(length):
-        @pl.when(spot - t >= 0)
-        def _():
-            if t:
-                arrive((spot - t) * 2 + side)
-
-            @pl.when(has_right)
+        for h in range(PARTS):
+            @pl.when(spot - t >= 0)
             def _():
-                to_right(t).start()
-
-            if t:
-                across(spot - t).start()
-
-        @pl.when(spot + t < length)
-        def _():
-            if t:
-                arrive((spot + t) * 2 + side)
-
-            @pl.when(has_left)
+                if t:
+                    arrive((spot - t) * 2 + side, h)
+
+                @pl.when(has_right)
+                def _():
+                    to_right(t, h).start()
+
+                if t:
+                    across(spot - t, h).start()
+
+            @pl.when(spot + t < length)
             def _():
-                to_left(t).start()
-
-            across(spot + t).start()
-
-    for at in range(length):
-        arrive(at * 2 + 1 - side)
-        across(at).wait_send()
-    for t in range(length):
-        @pl.when((spot - t >= 0) & has_right)
-        def _():
-            to_right(t).wait_send()
-
-        @pl.when((spot + t < length) & has_left)
-        def _():
-            to_left(t).wait_send()
+                if t:
+                    arrive((spot + t) * 2 + side, h)
+
+                @pl.when(has_left)
+                def _():
+                    to_left(t, h).start()
+
+                across(spot + t, h).start()
+
+    for h in range(PARTS):
+        for at in range(length):
+            arrive(at * 2 + 1 - side, h)
+            across(at, h).wait_send()
+        for t in range(length):
+            @pl.when((spot - t >= 0) & has_right)
+            def _():
+                to_right(t, h).wait_send()
+
+            @pl.when((spot + t < length) & has_left)
+            def _():
+                to_left(t, h).wait_send()
 
 
 def line_sems():
     n = lax.axis_size("dp")
     dma = pltpu.SemaphoreType.DMA
-    return [dma((n // 2,)), dma((n // 2,)), dma((n // 2,)), dma((n,))]
+    return [dma((n // 2, PARTS)), dma((n // 2, PARTS)), dma((n // 2, PARTS)), dma((n, PARTS))]
 
 
 def gather_kernel(q_ref, all_ref, own_sem, *sems):

time: 121 us -> 117 us (0.967)
  Pallas kernels: 112 us -> 109 us
    pallas_call x1, Pallas kernels: 60.2 us -> 56.1 us  [finish(): pl.pallas_call(finish_kernel, out_shape=(jax.ShapeDtypeStruct((rows, q_lo...]
    pallas_call x1, Pallas kernels: 28.6 us -> 30.8 us  [attend(): pl.pallas_call(functools.partial(attend_kernel, sizes), out_shape=(jax.Sh...]
    pallas_call x1, Pallas kernels: 23.5 us -> 21.9 us  [gather_queries(): pl.pallas_call(gather_kernel, out_shape=jax.ShapeDtypeStruct((n,) + queri...]
where the time goes in v4:
time: 117 us; the launch traced here: 116 us
  Pallas kernels  109 us (93%)
  local copies, waits for them, and re-layouts  4.03 us (3%)
  other arithmetic  2.57 us (2%)
    pallas_call x1, Pallas kernels, finish(): pl.pallas_call(finish_kernel, out_shape=(jax.ShapeDtypeStruct((rows, q_lo...  56.1 us
    pallas_call x1, Pallas kernels, attend(): pl.pallas_call(functools.partial(attend_kernel, sizes), out_shape=(jax.Sh...  30.8 us
    pallas_call x1, Pallas kernels, gather_queries(): pl.pallas_call(gather_kernel, out_shape=jax.ShapeDtypeStruct((n,) + queri...  21.9 us
    unnamed x4, local copies, waits for them, and re-layouts  3.14 us

profile of v4, /device:TPU:0, one launch (start us, length us, event | category | flops | bytes accessed | tf_op | source)
XLA Modules:
  0.0 116.3 jit_solution(8074992989752064577)
XLA Ops:
  0.6 0.9 convert_reduce_fusion
  1.5 0.0 copy-start
  1.5 0.1 min.22
  1.6 0.7 reduce_sum.29.totals
  2.3 0.8 add_select_fusion
  3.2 0.2 fusion
  3.4 0.2 select_reduce_fusion
  3.5 0.1 copy.12
  3.6 0.7 reshape.25.codes
  4.3 21.9 %shard_map.77.q_ref = bf16[8,32,16,128]{3,2,1,0:T(8,128)(2,1)} custom-call(bf16[32,16,128]{2,1,0:T(8,128)(2,1)} %q_ref.1), custom_call_target="tpu_custom_call" | custom-call | tf_op jit(solution)/shard_map/pallas_call | solution.py:116
  26.2 0.0 copy-done
  26.2 30.8 %shard_map.78 = (s16[8,32,16,128]{3,2,1,0:T(8,128)(2,1)}, f32[8,3,16,128]{3,2,1,0:T(8,128)}) custom-call(s32[8192]{0:T(1024)} %reshape.25.codes, s32[256]{0:T(256)} %copy-done, s32[8]{0:T(128)} %reduce_sum.29.totals, bf16[8,32,16,128]{3,2,1,0:T(8,128)(2,1)} %shard_map.77.q_ref, bf16[1024,32,128]{2,1,0:T(8,128)(2,1)} %bitcast.3, bf16[1024,32,128]{2,1,0:T(8,128)(2,1)} %bitcast.4), custom_call_target="tpu_custom_call" | custom-call | tf_op jit(solution)/shard_map/pallas_call | solution.py:299
  57.0 56.1 %shard_map.79 = (bf16[32,16,128]{2,1,0:T(8,128)(2,1)}, bf16[64,1024]{1,0:T(8,128)(2,1)}) custom-call(s16[8,32,16,128]{3,2,1,0:T(8,128)(2,1)} %get-tuple-element.4.acc_hbm, f32[8,3,16,128]{3,2,1,0:T(8,128)} %get-tuple-element.5.stat_hbm, bf16[2048,1024]{1,0:T(8,128)(2,1)} %w_hbm.1), custom_call_target="tpu_custom_call" | custom-call | tf_op jit(solution)/shard_map/pallas_call | solution.py:444
  113.2 1.6 %copy.19 = bf16[32,16,128]{2,1,0:T(8,128)(2,1)} copy(bf16[32,16,128]{2,1,0:T(8,128)(2,1)} %get-tuple-element.10) | data formatting | bytes 262144
  114.7 1.6 %copy.20 = bf16[64,1024]{1,0:T(8,128)(2,1)} copy(bf16[64,1024]{1,0:T(8,128)(2,1)} %get-tuple-element.11) | data formatting | bytes 262144
  (2 shorter events, 0.0 us)
Async XLA Ops:
  1.5 24.7 %copy-start = (s32[256]{0:T(256)}, s32[256]{0:T(256)S(1)}, u32[]{:S(2)}) copy-start(s32[256]{0:T(256)S(1)} %get-tuple-element.6.counts) | copy-start | bytes 3076
